TPU v7x, 32 devices: a whole 2x2x4 slice. The times are simulated.
32 devices in a mesh: elem: 16 (over z, y, x), param: 2 (over core).
Axes of the slice: x: 2, y: 2, z: 4, core: 2. Of those that a mesh axis runs over, the one named last changes fastest.
Arguments:
- coords: bfloat16 [8, 300], P('param'), may hold values from -6 to 6
- basis_rows: bfloat16 [3, 300, 4096], P(None, None, 'elem'), may hold values from -0.375 to 0.375
- connectivity: int32 [4096, 8], P(('elem', 'param')), may hold values from 0 to 319, as said below
- modulus: float32 [4096], P(('elem', 'param')), may hold values from 0.5 to 15
- stiffness: float32 [24, 24], replicated, may hold values from -1.25 to 1.25
Outputs:
- training: bfloat16 [8, 300, 4096], P(None, None, ('elem', 'param'))
- target: float32 [8, 300], replicated
Inputs may be any that keep to these rules, and one draw needn't show every extreme that they name: `connectivity`: A number c of 256 or more names node c - 256 of the next node block; the last block's next block is the first. An element's eight corner numbers lie among min(8, 64) consecutive numbers; where these lie in the block is not tied to the element's position.
All inputs are finite; a program needn't handle non-finite values.
Results may differ from a plain program's by a relative error of at most 0.0072.
Values may be sent and summed in bfloat16 or wider, within the bound.
A program may use at most 64 MiB of HBM per device.

v0:
```python
import math

import jax
import jax.numpy as jnp
from jax import lax
from jax.sharding import PartitionSpec as P


def passed_along(value, axis, by):
    peers = lax.axis_size(axis)
    return lax.ppermute(value, axis, [(i, (i + by) % peers) for i in range(peers)])


def local(coords, basis_rows, connectivity, modulus, stiffness):
    node_count = basis_rows.shape[2]
    ghost_count = node_count // 4
    ghost_rows = passed_along(basis_rows[:, :, :ghost_count], "elem", -1)
    extended = jnp.concatenate([basis_rows, ghost_rows], axis=2)
    corner_ids = connectivity.T
    elem_count = corner_ids.shape[1]
    element_basis = extended[:, :, corner_ids]
    cycle_size = lax.axis_size("param")
    all_coords = lax.all_gather(coords, "param", axis=0, tiled=True)
    displaced = jnp.stack(
        [
            jnp.dot(all_coords, extended[component], preferred_element_type=jnp.float32)
            for component in range(3)
        ],
        axis=1,
    ).astype(jnp.bfloat16)
    snaps = displaced.shape[0]
    corner_disp = displaced[:, :, corner_ids].reshape(snaps, 24, elem_count).astype(jnp.float32)
    linear = jnp.einsum("kj,sje->ske", stiffness, corner_disp, precision=lax.Precision.HIGHEST)
    forces = (modulus * (linear + 0.25 * corner_disp * corner_disp * corner_disp)).astype(
        jnp.bfloat16
    )
    forces = forces.reshape(snaps, 3, 8, elem_count)
    matrix = jnp.einsum("cmae,scae->sme", element_basis, forces, preferred_element_type=jnp.float32)
    norm_sums = jnp.sum(jnp.sqrt(jnp.sum(matrix * matrix, axis=1)), axis=1)
    force_sums = jnp.sum(matrix, axis=2)
    norm_sums, force_sums = lax.psum((norm_sums, force_sums), ("elem", "param"))
    elem_total = elem_count * lax.axis_size("elem") * cycle_size
    row_scale = norm_sums / elem_total
    target = force_sums / (row_scale[:, None] * math.sqrt(elem_total))
    training = (matrix / row_scale[:, None, None]).astype(jnp.bfloat16)
    return (training, target)


def solution(mesh):
    in_specs = (
        P("param", None),
        P(None, None, "elem"),
        P(("elem", "param"), None),
        P(("elem", "param")),
        P(),
    )
    out_specs = (P(None, None, ("elem", "param")), P())
    return jax.shard_map(local, mesh=mesh, in_specs=in_specs, out_specs=out_specs, check_vma=False)
```

profile of v0, /device:TPU:0, one launch (start us, length us, event | category | flops | bytes accessed | tf_op | source)
XLA Modules:
  0.0 81.1 jit_solution(3763947510035681350)
XLA Ops:
  0.6 1.5 %copy.29 = bf16[3,300,256]{1,0,2:T(4,128)(2,1)S(1)} copy(bf16[3,300,256]{2,1,0:T(8,128)(2,1)} %param.6) | data formatting | bytes 921600 | tf_op args[1]
  2.2 7.0 %collective-permute-start = (bf16[3,300,64]{1,0,2:T(4,128)(2,1)S(1)}, bf16[3,300,64]{1,0,2:T(4,128)(2,1)S(1)}, u32[]{:S(2)}, u32[]{:S(2)}) collective-permute-start(bf16[3,300,64]{1,0,2:T(4,128)(2,1)S(1)} %slice.20), channel_id=1, source_target_pairs={{0,30},{2,0},{4,2},{6,4},{8,6},{10,8},{12,10},{14,12},{16,14},{18,... | collective-permute-start | bytes 345608 | tf_op jit(solution)/shard_map/ppermute | solution.py:11
  9.2 1.9 %all-gather = bf16[2,4,300]{2,1,0:T(4,128)(2,1)S(1)} all-gather(bf16[1,4,300]{2,1,0:T(4,128)(2,1)} %bitcast.72), channel_id=1, replica_groups=mesh['elem'=16,'param'=2] {'param'}, dimensions={0}, use_global_device_ids=true | all-gather | bytes 7200 | tf_op jit(solution)/shard_map/all_gather | solution.py:23
  11.2 0.7 fusion.21
  11.9 1.5 %collective-permute-done = bf16[3,300,64]{1,0,2:T(4,128)(2,1)S(1)} collective-permute-done((bf16[3,300,64]{1,0,2:T(4,128)(2,1)S(1)}, bf16[3,300,64]{1,0,2:T(4,128)(2,1)S(1)}, u32[]{:S(2)}, u32[]{:S(2)}) %collective-permute-start) | collective-permute-done | bytes 115232 | tf_op jit(solution)/shard_map/ppermute | solution.py:11
  13.4 2.1 %fusion.12 = (bf16[1,300,320]{1,0,2:T(2,128)(2,1)S(1)}, bf16[1,300,320]{1,0,2:T(2,128)(2,1)S(1)}, bf16[1,300,320]{1,0,2:T(2,128)(2,1)S(1)}) fusion(bf16[3,300,256]{1,0,2:T(4,128)(2,1)S(1)} %copy.29, bf16[3,300,64]{1,0,2:T(4,128)(2,1)S(1)} %collective-permute-done), kind=kLoop, calls=%fused_computation.28 | loop fusion | flops 288000 | bytes 1152000 | tf_op jit(solution)/shard_map/concatenate | solution.py:18
  15.5 0.9 %copy.30 = bf16[1,300,320]{2,1,0:T(8,128)(2,1)S(1)} copy(bf16[1,300,320]{1,0,2:T(2,128)(2,1)S(1)} %get-tuple-element.14) | data formatting | bytes 384000 | tf_op jit(solution)/shard_map/slice | solution.py:26
  16.3 0.9 %copy.31 = bf16[1,300,320]{2,1,0:T(8,128)(2,1)S(1)} copy(bf16[1,300,320]{1,0,2:T(2,128)(2,1)S(1)} %get-tuple-element.15) | data formatting | bytes 384000 | tf_op jit(solution)/shard_map/slice | solution.py:26
  17.2 0.1 fusion.9
  17.4 0.2 fusion.10
  17.5 0.9 %copy.32 = bf16[1,300,320]{2,1,0:T(8,128)(2,1)S(1)} copy(bf16[1,300,320]{1,0,2:T(2,128)(2,1)S(1)} %get-tuple-element.16) | data formatting | bytes 384000 | tf_op jit(solution)/shard_map/slice | solution.py:26
  18.4 0.1 fusion.11
  18.5 0.2 copy.33
  18.8 3.6 %gather_fusion = bf16[1024,8,3]{1,2,0:T(4,128)(2,1)S(1)} fusion(bf16[8,3,320]{0,1,2:T(4,128)(2,1)S(1)} %copy.33, s32[1024]{0:T(1024)S(1)} %fusion.21), kind=kCustom, calls=%fused_computation | custom fusion | bytes 102400 | tf_op jit(solution)/shard_map/gather | solution.py:32
  22.4 0.5 copy.34
  22.9 0.2 fusion.8
  23.0 0.4 copy.36
  23.5 0.7 pad_maximum_fusion
  24.2 9.9 %gather_fusion.1 = bf16[1024,3,300]{2,1,0:T(4,128)(2,1)} fusion(bf16[3,300,320]{1,0,2:T(4,128)(2,1)S(1)} %pad_maximum_fusion, s32[1024]{0:T(1024)S(1)} %fusion.21), kind=kCustom, calls=%fused_computation.1 | custom fusion | bytes 3690496 | tf_op jit(solution)/shard_map/gather | solution.py:21
  34.1 4.0 %bitcast_reduce_fusion = (f32[8,300]{1,0:T(8,128)S(1)}, f32[8,128]{0,1:T(8,128)S(1)}, f32[128,8,300,1]{2,1,3,0:T(8,128)S(1)}) fusion(bf16[8,3,8,128]{2,0,1,3:T(8,128)(2,1)S(1)} %copy.36, bf16[8,128,3,300]{3,2,1,0:T(4,128)(2,1)} %bitcast.71), kind=kOutput, calls=%fused_computation.5 | convolution fusion | flops 15663776 | bytes 3134848 | tf_op jit(solution)/shard_map/cmae,scae->sme/dot_general | solution.py:38
  38.1 40.7 %all-reduce = (f32[8]{0:T(128)S(1)}, f32[8,300]{1,0:T(8,128)S(1)}) all-reduce(f32[8]{0:T(128)S(1)} %sqrt_reduce_fusion, f32[8,300]{1,0:T(8,128)S(1)} %get-tuple-element.10), channel_id=1, replica_groups=mesh['elem'=16,'param'=2] {'elem','param'}, use_global_device_ids=true, to_apply=%region_2.0 | all-reduce | flops 2408 | bytes 19264 | tf_op jit(solution)/shard_map/psum | solution.py:41
  78.8 0.2 fusion.4
  79.0 1.5 %copy.37 = bf16[8,300,128]{2,0,1:T(8,128)(2,1)} copy(bf16[8,300,128]{1,0,2:T(8,128)(2,1)S(1)} %fusion.4) | data formatting | bytes 1228800
  80.4 0.7 broadcast_divide_fusion
  (9 shorter events, 0.2 us)
Async XLA Ops:
  0.6 22.2 %copy-start = (f32[24,24]{1,0:T(8,128)S(1)}, f32[24,24]{1,0:T(8,128)}, u32[]{:S(2)}) copy-start(f32[24,24]{1,0:T(8,128)} %param.9) | copy-start | bytes 6916
  2.2 11.2 %collective-permute-start = (bf16[3,300,64]{1,0,2:T(4,128)(2,1)S(1)}, bf16[3,300,64]{1,0,2:T(4,128)(2,1)S(1)}, u32[]{:S(2)}, u32[]{:S(2)}) collective-permute-start(bf16[3,300,64]{1,0,2:T(4,128)(2,1)S(1)} %slice.20), channel_id=1, source_target_pairs={{0,30},{2,0},{4,2},{6,4},{8,6},{10,8},{12,10},{14,12},{16,14},{18,... | collective-permute-start | bytes 345608 | tf_op jit(solution)/shard_map/ppermute | solution.py:11
  15.5 7.4 %copy-start.1 = (f32[128]{0:T(128)S(1)}, f32[128]{0:T(128)}, u32[]{:S(2)}) copy-start(f32[128]{0:T(128)} %param.8) | copy-start | bytes 1540
where the time goes:
time: 81.4 us; the launch traced here: 81.1 us
  blocking collectives  42.6 us (52%)
  local copies, waits for them, and re-layouts  20.2 us (25%)
  starting transfers between devices  7.01 us (9%)
  matrix products  4.59 us (6%)
  other arithmetic  4.38 us (5%)
  waiting for transfers between devices  1.51 us (2%)
    psum x1, blocking collectives, local(): norm_sums, force_sums = lax.psum((norm_sums, force_sums), ('elem', 'param'))  40.7 us
    gather x1, local copies, waits for them, and re-layouts, local(): element_basis = extended[:, :, corner_ids]  9.92 us
    ppermute x1, starting transfers between devices, passed_along(): lax.ppermute(value, axis, [(i, (i + by) % peers) for i in range(peers)])  7.01 us
    gather x2, local copies, waits for them, and re-layouts, local(): displaced[:, :, corner_ids].reshape(snaps, 24, elem_count)  4.05 us
    dot_general x1, matrix products, local(): jnp.einsum('cmae,scae->sme', element_basis, forces, preferred_element_typ...  3.98 us
    unnamed x7, local copies, waits for them, and re-layouts  2.95 us
    concatenate x2, other arithmetic, local(): extended = jnp.concatenate([basis_rows, ghost_rows], axis=2)  2.76 us
    slice x3, local copies, waits for them, and re-layouts, local(): extended[component]  2.6 us
  transfers between devices with their start and end apart: 1, of which 1 were waited for; matrix products, arithmetic and copies ran while one was open for 1% of the time, Pallas kernels for 0%

commit v1 on v0

v1 whole, which is shorter than its diff:
```python
import functools
import math

import jax
import jax.numpy as jnp
from jax import lax
from jax.experimental import pallas as pl
from jax.experimental.pallas import tpu as pltpu
from jax.sharding import PartitionSpec as P

MESH = pl.DeviceIdType.MESH
F32 = jnp.float32
BF16 = jnp.bfloat16


def round_up(value, to):
    return -(-value // to) * to


def kernel(
    elems, params, inner,
    coords_ref, basis_ref, conn_ref, mod_ref, stiff_ref,
    cols_ref, target_ref, scale_ref,
    packed, ghost_in, ghost, all_coords, disp, mask, weights, part, part_p, part_i, part_o,
    send_g, recv_g, send_c, recv_c, send_p, recv_p, send_i, recv_i, send_o, recv_o,
):
    outer = elems // inner
    own_snaps, modes = coords_ref.shape
    snaps = own_snaps * params
    nodes = basis_ref.shape[2]
    ghosts = nodes // 4
    total_nodes = nodes + ghosts
    count = conn_ref.shape[0]
    me_e, me_p = lax.axis_index("elem"), lax.axis_index("param")
    me_i, me_o = me_e % inner, me_e // inner
    before, after = (me_e + elems - 1) % elems, (me_e + 1) % elems

    def peers(me, size):
        return [((me + j) % size, (me + size - j) % size) for j in range(1, size)]

    def inner_id(i):
        return (me_o * inner + i, me_p)

    def outer_id(o):
        return (o * inner + me_i, me_p)

    barrier = pltpu.get_barrier_semaphore()
    near = [(before, me_p), (after, me_p)]
    near += [(me_e, to) for to, _ in peers(me_p, params)]
    near += [inner_id(to) for to, _ in peers(me_i, inner)]
    near += [outer_id(to) for to, _ in peers(me_o, outer)]
    for device in near:
        pl.semaphore_signal(barrier, inc=1, device_id=device, device_id_type=MESH)

    half = packed.shape[1]
    split = half < modes
    if split:
        for k in range(3):
            packed[k, :, :ghosts] = basis_ref[k, :half, :ghosts]
            packed[k, : modes - half, ghosts:] = basis_ref[k, half:, :ghosts]
    else:
        for k in range(3):
            packed[k, :modes] = basis_ref[k, :, :ghosts]
    padded = all_coords.shape[2]
    all_coords[me_p, :own_snaps, :modes] = coords_ref[...].astype(F32)

    pl.semaphore_wait(barrier, len(near))
    ghost_copy = pltpu.make_async_remote_copy(
        src_ref=packed, dst_ref=ghost_in, send_sem=send_g, recv_sem=recv_g,
        device_id=(before, me_p), device_id_type=MESH,
    )
    ghost_copy.start()

    def exchange(ref, me, size, device_of, send, recv):
        copies = []
        for j, (to, source) in enumerate(peers(me, size)):
            out = pltpu.make_async_remote_copy(
                src_ref=ref.at[me], dst_ref=ref.at[me], send_sem=send.at[j], recv_sem=recv.at[me],
                device_id=device_of(to), device_id_type=MESH,
            )
            out.start()
            came = pltpu.make_async_remote_copy(
                src_ref=ref.at[source], dst_ref=ref.at[source], send_sem=send.at[j],
                recv_sem=recv.at[source], device_id=device_of(to), device_id_type=MESH,
            )
            copies.append((out, came))
        return copies

    def finish(copies):
        for out, came in copies:
            came.wait_recv()
        for out, came in copies:
            out.wait_send()

    coord_copies = exchange(all_coords, me_p, params, lambda p: (me_e, p), send_c, recv_c)

    corners = jnp.transpose(conn_ref[...])
    base = jnp.min(corners, axis=0, keepdims=True)
    residue = corners % 8
    lane_at = corners % 128
    tile_at = corners // 128
    node = lax.broadcasted_iota(jnp.int32, (total_nodes, count), 0)
    inside = (node >= base) & (node < base + 8)
    mask[...] = jnp.where(inside, 1.0, 0.0).astype(BF16)
    stiff = stiff_ref[...]
    high = stiff.astype(BF16)
    rest = stiff - high.astype(F32)
    mid = rest.astype(BF16)
    low = (rest - mid.astype(F32)).astype(BF16)
    modulus = mod_ref[...]
    modulus2 = jnp.concatenate([modulus, modulus], axis=1)

    finish(coord_copies)
    full_coords = jnp.concatenate(
        [all_coords[p, :own_snaps, :modes] for p in range(params)], axis=0
    ).astype(BF16)
    own_tiles = nodes // 128
    for k in range(3):
        moved = jnp.dot(full_coords, basis_ref[k], preferred_element_type=F32)
        moved = moved.astype(BF16).astype(F32)
        for t in range(own_tiles):
            disp[t, k] = moved[:, t * 128 : (t + 1) * 128]

    ghost_copy.wait_recv()
    for k in range(3):
        if split:
            ghost[:half, k * ghosts : (k + 1) * ghosts] = ghost_in[k, :, :ghosts]
            ghost[half:, k * ghosts : (k + 1) * ghosts] = ghost_in[k, : modes - half, ghosts:]
        else:
            ghost[:, k * ghosts : (k + 1) * ghosts] = ghost_in[k, :modes]
    moved = jnp.dot(full_coords, ghost[...], preferred_element_type=F32).astype(BF16).astype(F32)
    ghost_tiles = disp.shape[0] - own_tiles
    for k in range(3):
        for t in range(ghost_tiles):
            width = min(128, ghosts)
            disp[own_tiles + t, k, :, :width] = moved[:, k * ghosts + t * 128 :][:, :width]

    lane = lax.broadcasted_iota(jnp.int32, (1, 128), 1)
    row8 = lax.broadcasted_iota(jnp.int32, (8, count), 0)

    def one_pair(p, sums):
        pieces = []
        for at in range(2):
            rows = []
            for k in range(3):
                found = jnp.zeros((8, count), F32)
                for t in range(disp.shape[0]):
                    line = jnp.broadcast_to(disp[t, k, pl.ds(2 * p + at, 1), :], (8, 128))
                    got = jnp.take_along_axis(line, lane_at, axis=1)
                    found = jnp.where(tile_at == t, got, found)
                rows.append(found)
            pieces.append(jnp.concatenate(rows, axis=0))
        moved = jnp.concatenate(pieces, axis=1)
        moved16 = moved.astype(BF16)
        linear = jnp.dot(low, moved16, preferred_element_type=F32)
        linear = linear + jnp.dot(mid, moved16, preferred_element_type=F32)
        linear = linear + jnp.dot(high, moved16, preferred_element_type=F32)
        forces = (modulus2 * (linear + 0.25 * moved * moved * moved)).astype(BF16).astype(F32)
        for at in range(2):
            for k in range(3):
                spread = jnp.zeros((8, count), F32)
                for a in range(8):
                    force = forces[k * 8 + a : k * 8 + a + 1, at * count : (at + 1) * count]
                    spread = spread + jnp.where(residue[a : a + 1] == row8, force, 0.0)
                twice = jnp.concatenate([spread, spread], axis=0).astype(BF16)
                tall = jnp.concatenate([twice] * (total_nodes // 16), axis=0) * mask[...]
                columns = slice(at * count, (at + 1) * count)
                weights[k * nodes : (k + 1) * nodes, columns] = tall[:nodes]
                start = 3 * nodes + k * ghosts
                weights[start : start + ghosts, columns] = tall[nodes:]
        result = jnp.dot(ghost[...], weights[3 * nodes :], preferred_element_type=F32)
        for k in range(3):
            result = result + jnp.dot(
                basis_ref[k], weights[k * nodes : (k + 1) * nodes], preferred_element_type=F32
            )
        for at in range(2):
            s = 2 * p + at
            mine = result[:, at * count : (at + 1) * count]
            cols_ref[s] = mine
            norm = jnp.sqrt(jnp.sum(mine * mine, axis=0, keepdims=True))
            norm = jnp.sum(norm, axis=1, keepdims=True)
            line = jnp.concatenate([jnp.sum(mine, axis=1, keepdims=True), norm], axis=0)
            sums = jnp.where(lane == s, line, sums)
        return sums

    sums = jnp.zeros((modes + 1, 128), F32)
    if snaps <= 8:
        for p in range(snaps // 2):
            sums = one_pair(p, sums)
    else:
        sums = lax.fori_loop(0, snaps // 2, one_pair, sums)
    wide = part_p.shape[2]
    part[...] = jnp.zeros_like(part)
    part[: modes + 1] = sums
    flat = jnp.concatenate(
        [jnp.transpose(part[t * 128 : (t + 1) * 128])[:snaps] for t in range(wide // 128)], axis=1
    )
    ghost_copy.wait_send()

    def reduced(value, ref, me, size, device_of, send, recv):
        ref[me] = value
        finish(exchange(ref, me, size, device_of, send, recv))
        total = ref[0]
        for j in range(1, size):
            total = total + ref[j]
        return total

    flat = reduced(flat, part_p, me_p, params, lambda p: (me_e, p), send_p, recv_p)
    flat = reduced(flat, part_i, me_i, inner, inner_id, send_i, recv_i)
    flat = reduced(flat, part_o, me_o, outer, outer_id, send_o, recv_o)
    elem_total = count * elems * params
    row_scale = flat[:, modes : modes + 1] / elem_total
    target_ref[...] = flat[:, :modes] / (row_scale * math.sqrt(elem_total))
    scale_ref[...] = jnp.broadcast_to(1.0 / row_scale, scale_ref.shape)


def local(elems, params, coords, basis_rows, connectivity, modulus, stiffness):
    own_snaps, modes = coords.shape
    nodes = basis_rows.shape[2]
    count = connectivity.shape[0]
    snaps = own_snaps * params
    ghosts = nodes // 4
    inner = 4 if elems % 4 == 0 else elems
    outer = elems // inner
    half, across = (modes, ghosts) if ghosts % 128 == 0 else (round_up(-(-modes // 2), 32), 2 * ghosts)
    tall = round_up(half, 16)
    tiles = nodes // 128 + -(-ghosts // 128)
    wide = round_up(modes + 1, 128)
    dma = pltpu.SemaphoreType.DMA
    vmem = pl.BlockSpec(memory_space=pltpu.VMEM)
    cols, target, scale = pl.pallas_call(
        functools.partial(kernel, elems, params, inner),
        out_shape=(
            jax.ShapeDtypeStruct((snaps, modes, count), F32),
            jax.ShapeDtypeStruct((snaps, modes), F32),
            jax.ShapeDtypeStruct((snaps, 128), F32),
        ),
        in_specs=[vmem] * 5,
        out_specs=(vmem, vmem, vmem),
        scratch_shapes=[
            pltpu.VMEM((3, tall, across), BF16),
            pltpu.VMEM((3, tall, across), BF16),
            pltpu.VMEM((modes, 3 * ghosts), BF16),
            pltpu.VMEM((params, round_up(own_snaps, 8), round_up(modes, 128)), F32),
            pltpu.VMEM((tiles, 3, snaps, 128), F32),
            pltpu.VMEM((nodes + ghosts, count), BF16),
            pltpu.VMEM((3 * (nodes + ghosts), 2 * count), BF16),
            pltpu.VMEM((wide, 128), F32),
            pltpu.VMEM((params, snaps, wide), F32),
            pltpu.VMEM((inner, snaps, wide), F32),
            pltpu.VMEM((outer, snaps, wide), F32),
            dma, dma,
            dma((params,)), dma((params,)),
            dma((params,)), dma((params,)),
            dma((inner,)), dma((inner,)),
            dma((outer,)), dma((outer,)),
        ],
        compiler_params=pltpu.CompilerParams(
            collective_id=0, has_side_effects=True, vmem_limit_bytes=48 * 1024 * 1024
        ),
    )(coords, basis_rows, connectivity, modulus.reshape(1, count), stiffness)
    training = (cols * scale[:, :1, None]).astype(BF16)
    return (training, target)


def solution(mesh):
    in_specs = (
        P("param", None),
        P(None, None, "elem"),
        P(("elem", "param"), None),
        P(("elem", "param")),
        P(),
    )
    out_specs = (P(None, None, ("elem", "param")), P())
    run = functools.partial(local, mesh.shape["elem"], mesh.shape["param"])
    return jax.shard_map(run, mesh=mesh, in_specs=in_specs, out_specs=out_specs, check_vma=False)
```

time: 81.4 us -> 29.7 us (0.36)
  blocking collectives: 42.6 us -> 0 us
  Pallas kernels: 0 us -> 23.1 us
  local copies, waits for them, and re-layouts: 20.2 us -> 5.55 us
  starting transfers between devices: 7.01 us -> 0 us
  matrix products: 4.59 us -> 0 us
  other arithmetic: 4.38 us -> 0.17 us
  waiting for transfers between devices: 1.51 us -> 0 us
    psum x1 -> x0, blocking collectives: 40.7 us -> none  [local(): norm_sums, force_sums = lax.psum((norm_sums, force_sums), ('elem', 'param'))]
    pallas_call x0 -> x1, Pallas kernels: none -> 23.1 us  [local(): pl.pallas_call(functools.partial(kernel, elems, params, inner), out_shape...]
    gather x3 -> x0, local copies, waits for them, and re-layouts: 14 us -> none  [the longest x1 9.92 us: local(): element_basis = extended[:, :, corner_ids]]
    ppermute x1 -> x0, starting transfers between devices: 7.01 us -> none  [passed_along(): lax.ppermute(value, axis, [(i, (i + by) % peers) for i in range(peers)])]
    dot_general x5 -> x0, matrix products: 4.59 us -> none  [the longest x1 3.98 us: local(): jnp.einsum('cmae,scae->sme', element_basis, forces, preferred_element_typ...]
    concatenate x2 -> x0, other arithmetic: 2.76 us -> none  [local(): extended = jnp.concatenate([basis_rows, ghost_rows], axis=2)]
    slice x4 -> x1, local copies, waits for them, and re-layouts: 2.67 us -> 0.11 us  [local(): training = (cols * scale[:, :1, None]).astype(BF16)]
    unnamed x7 -> x11, local copies, waits for them, and re-layouts: 2.95 us -> 5.43 us
  transfers between devices with their start and end apart: 1 -> 0, of which waited for: 1 -> 0; matrix products, arithmetic and copies ran while one was open for 1% -> 0% of each run, Pallas kernels for 0% -> 0%
where the time goes in v1:
time: 29.7 us; the launch traced here: 29.4 us
  Pallas kernels  23.1 us (78%)
  local copies, waits for them, and re-layouts  5.55 us (19%)
  between operations  0.65 us (2%)
    pallas_call x1, Pallas kernels, local(): pl.pallas_call(functools.partial(kernel, elems, params, inner), out_shape...  23.1 us
    unnamed x11, local copies, waits for them, and re-layouts  5.43 us

profile of v1, /device:TPU:0, one launch (start us, length us, event | category | flops | bytes accessed | tf_op | source)
XLA Modules:
  0.0 29.4 jit_solution(2964734642635859559)
XLA Ops:
  0.6 0.8 %copy.9.conn_ref = s32[128,8]{1,0:T(8,128)S(1)} copy(s32[128,8]{0,1:T(8,128)} %param.7) | data formatting | bytes 8192 | tf_op args[2]
  1.4 0.0 copy-start
  1.4 1.0 %copy-done = bf16[3,300,256]{2,1,0:T(8,128)(2,1)S(1)} copy-done((bf16[3,300,256]{2,1,0:T(8,128)(2,1)S(1)}, bf16[3,300,256]{2,1,0:T(8,128)(2,1)}, u32[]{:S(2)}) %copy-start) | copy-done | bytes 460824
  2.4 0.0 copy-start.1
  2.4 0.7 %copy-done.1 = f32[24,24]{1,0:T(8,128)S(1)} copy-done((f32[24,24]{1,0:T(8,128)S(1)}, f32[24,24]{1,0:T(8,128)}, u32[]{:S(2)}) %copy-start.1) | copy-done | bytes 2328
  3.1 0.0 copy-start.2
  3.1 0.7 %copy-done.2 = bf16[4,300]{1,0:T(4,128)(2,1)S(1)} copy-done((bf16[4,300]{1,0:T(4,128)(2,1)S(1)}, bf16[4,300]{1,0:T(4,128)(2,1)}, u32[]{:S(2)}) %copy-start.2) | copy-done | bytes 2424
  3.8 0.0 copy-start.3
  3.8 0.7 %copy-done.3 = f32[128]{0:T(128)S(1)} copy-done((f32[128]{0:T(128)S(1)}, f32[128]{0:T(128)}, u32[]{:S(2)}) %copy-start.3) | copy-done | bytes 536
  4.5 23.1 %shard_map.68 = (f32[8,300,128]{2,1,0:T(8,128)S(1)}, f32[8,300]{1,0:T(8,128)S(1)}, f32[8,128]{1,0:T(8,128)S(1)}) custom-call(bf16[4,300]{1,0:T(4,128)(2,1)S(1)} %copy-done.2, bf16[3,300,256]{2,1,0:T(8,128)(2,1)S(1)} %copy-done, s32[128,8]{1,0:T(8,128)S(1)} %copy.9.conn_ref, f32[1,128]{1,0:T(1,128)S(1)} %bitcast.1, f32[24,24]{1,0:T(8,128)S(1)} %copy-done.1), custom_call_target="tpu_custom_call" | custom-call | tf_op jit(solution)/shard_map/pallas_call | solution.py:231
  27.6 0.1 slice_reduce_fusion
  27.7 0.2 multiply_convert_fusion
  27.9 1.0 %copy.10 = bf16[8,300,128]{2,0,1:T(8,128)(2,1)} copy(bf16[8,300,128]{2,1,0:T(8,128)(2,1)S(1)} %multiply_convert_fusion) | data formatting | bytes 1228800
  28.8 0.6 %copy.12 = f32[8,300]{1,0:T(8,128)} copy(f32[8,300]{1,0:T(8,128)S(1)} %get-tuple-element.15) | data formatting | bytes 19200
Async XLA Ops:
  1.4 1.0 %copy-start = (bf16[3,300,256]{2,1,0:T(8,128)(2,1)S(1)}, bf16[3,300,256]{2,1,0:T(8,128)(2,1)}, u32[]{:S(2)}) copy-start(bf16[3,300,256]{2,1,0:T(8,128)(2,1)} %basis_ref.1) | copy-start | bytes 1382404
  2.4 0.7 %copy-start.1 = (f32[24,24]{1,0:T(8,128)S(1)}, f32[24,24]{1,0:T(8,128)}, u32[]{:S(2)}) copy-start(f32[24,24]{1,0:T(8,128)} %stiff_ref.1) | copy-start | bytes 6916
  3.1 0.7 %copy-start.2 = (bf16[4,300]{1,0:T(4,128)(2,1)S(1)}, bf16[4,300]{1,0:T(4,128)(2,1)}, u32[]{:S(2)}) copy-start(bf16[4,300]{1,0:T(4,128)(2,1)} %coords_ref.1) | copy-start | bytes 7204
  3.8 0.7 %copy-start.3 = (f32[128]{0:T(128)S(1)}, f32[128]{0:T(128)}, u32[]{:S(2)}) copy-start(f32[128]{0:T(128)} %param.8) | copy-start | bytes 1540

commit v2 on v1

v2 whole, which is shorter than its diff:
```python
import functools
import math

import jax
import jax.numpy as jnp
from jax import lax
from jax.experimental import pallas as pl
from jax.experimental.pallas import tpu as pltpu
from jax.sharding import PartitionSpec as P

MESH = pl.DeviceIdType.MESH
F32 = jnp.float32
BF16 = jnp.bfloat16


def round_up(value, to):
    return -(-value // to) * to


def kernel(
    elems, params, inner,
    coords_hbm, basis_hbm, conn_hbm, mod_hbm, stiff_hbm,
    cols_ref, flat_ref,
    coords_ref, basis_ref, conn_ref, mod_ref, stiff_ref,
    packed, ghost_in, ghost, disp, mask, weights, ghost_weights, acc, part, part_p, part_i, part_o,
    load, send_g, recv_g, send_d, recv_d, send_n, recv_n, send_p, recv_p, send_i, recv_i, send_o, recv_o,
):
    outer = elems // inner
    own_snaps, modes = coords_ref.shape
    snaps = own_snaps * params
    nodes = basis_hbm.shape[2]
    ghosts = nodes // 4
    total_nodes = nodes + ghosts
    count = conn_ref.shape[1]
    me_e, me_p = lax.axis_index("elem"), lax.axis_index("param")
    me_i, me_o = me_e % inner, me_e // inner
    before, after = (me_e + elems - 1) % elems, (me_e + 1) % elems

    def peers(me, size):
        return [((me + j) % size, (me + size - j) % size) for j in range(1, size)]

    def inner_id(i):
        return (me_o * inner + i, me_p)

    def outer_id(o):
        return (o * inner + me_i, me_p)

    barrier = pltpu.get_barrier_semaphore()
    near = [(before, p) for p in range(params)] + [(after, p) for p in range(params)]
    near += [(me_e, to) for to, _ in peers(me_p, params)]
    near += [inner_id(to) for to, _ in peers(me_i, inner)]
    near += [outer_id(to) for to, _ in peers(me_o, outer)]
    for device in near:
        pl.semaphore_signal(barrier, inc=1, device_id=device, device_id_type=MESH)

    loads = [(coords_hbm, coords_ref)]
    loads += [(basis_hbm.at[k], basis_ref.at[:, pl.ds(k * nodes, nodes)]) for k in range(3)]
    loads += [(conn_hbm, conn_ref), (mod_hbm, mod_ref), (stiff_hbm, stiff_ref)]
    loads = [pltpu.make_async_copy(src, dst, load.at[i]) for i, (src, dst) in enumerate(loads)]
    for copy in loads:
        copy.start()

    def remote(src, dst, send, recv, device):
        return pltpu.make_async_remote_copy(
            src_ref=src, dst_ref=dst, send_sem=send, recv_sem=recv,
            device_id=device, device_id_type=MESH,
        )

    own_tiles = nodes // 128
    ghost_tiles = disp.shape[1] - own_tiles
    half = packed.shape[1]
    split = half < modes
    loads[0].wait()
    for k in range(3):
        loads[1 + k].wait()
        moved = jnp.dot(
            coords_ref[...], basis_ref[:, k * nodes : (k + 1) * nodes], preferred_element_type=F32
        )
        moved = moved.astype(BF16).astype(F32)
        for t in range(own_tiles):
            disp[me_p, t, k] = moved[:, t * 128 : (t + 1) * 128]
    for k in range(3):
        at = k * nodes
        if split:
            packed[k, :, :ghosts] = basis_ref[:half, at : at + ghosts]
            packed[k, : modes - half, ghosts:] = basis_ref[half:, at : at + ghosts]
        else:
            packed[k, :modes] = basis_ref[:, at : at + ghosts]

    pl.semaphore_wait(barrier, len(near))
    own_part, ghost_part = pl.ds(0, own_tiles), pl.ds(own_tiles, ghost_tiles)
    sends, arrivals = [], []
    for p in range(params):
        turn = (me_p + p) % params
        source = (me_p + params - p) % params
        sends.append(remote(
            disp.at[me_p, pl.ds(0, ghost_tiles)], disp.at[me_p, ghost_part],
            send_d.at[p], recv_d.at[me_p], (before, turn),
        ))
        arrivals.append(remote(
            disp.at[source, pl.ds(0, ghost_tiles)], disp.at[source, ghost_part],
            send_d.at[p], recv_d.at[source], (before, turn),
        ))
        if p:
            sends.append(remote(
                disp.at[me_p, own_part], disp.at[me_p, own_part],
                send_n.at[p], recv_n.at[me_p], (me_e, turn),
            ))
            arrivals.append(remote(
                disp.at[source, own_part], disp.at[source, own_part],
                send_n.at[p], recv_n.at[source], (me_e, turn),
            ))
    ghost_copy = remote(packed, ghost_in, send_g, recv_g, (before, me_p))
    for copy in sends + [ghost_copy]:
        copy.start()

    for copy in loads[4:]:
        copy.wait()
    corners = conn_ref[...]
    base = jnp.min(corners, axis=0, keepdims=True)
    residue = corners % 8
    lane_at = corners % 128
    tile_at = corners // 128
    node = lax.broadcasted_iota(jnp.int32, (total_nodes, count), 0)
    inside = (node >= base) & (node < base + 8)
    mask[...] = jnp.where(inside, 1.0, 0.0).astype(BF16)
    stiff = stiff_ref[...]
    high = stiff.astype(BF16)
    rest = stiff - high.astype(F32)
    mid = rest.astype(BF16)
    low = (rest - mid.astype(F32)).astype(BF16)
    modulus = mod_ref[...]
    modulus2 = jnp.concatenate([modulus, modulus], axis=1)
    part[...] = jnp.zeros_like(part)
    lane = lax.broadcasted_iota(jnp.int32, (1, 128), 1)
    row8 = lax.broadcasted_iota(jnp.int32, (8, count), 0)

    for copy in arrivals:
        copy.wait_recv()

    def own_product(p):
        pieces = []
        for at in range(2):
            s = 2 * p + at
            rows = []
            for k in range(3):
                found = jnp.zeros((8, count), F32)
                for t in range(disp.shape[1]):
                    line = disp[s // own_snaps, t, k, pl.ds(s % own_snaps, 1), :]
                    got = jnp.take_along_axis(jnp.broadcast_to(line, (8, 128)), lane_at, axis=1)
                    found = jnp.where(tile_at == t, got, found)
                rows.append(found)
            pieces.append(jnp.concatenate(rows, axis=0))
        moved = jnp.concatenate(pieces, axis=1)
        moved16 = moved.astype(BF16)
        linear = jnp.dot(low, moved16, preferred_element_type=F32)
        linear = linear + jnp.dot(mid, moved16, preferred_element_type=F32)
        linear = linear + jnp.dot(high, moved16, preferred_element_type=F32)
        forces = (modulus2 * (linear + 0.25 * moved * moved * moved)).astype(BF16).astype(F32)
        for at in range(2):
            for k in range(3):
                spread = jnp.zeros((8, count), F32)
                for a in range(8):
                    force = forces[k * 8 + a : k * 8 + a + 1, at * count : (at + 1) * count]
                    spread = spread + jnp.where(residue[a : a + 1] == row8, force, 0.0)
                twice = jnp.concatenate([spread, spread], axis=0).astype(BF16)
                tall = jnp.concatenate([twice] * (total_nodes // 16), axis=0) * mask[...]
                columns = slice(at * count, (at + 1) * count)
                weights[k * nodes : (k + 1) * nodes, columns] = tall[:nodes]
                ghost_weights[p, k * ghosts : (k + 1) * ghosts, columns] = tall[nodes:]
        acc[p] = jnp.dot(basis_ref[...], weights[...], preferred_element_type=F32)

    def whole_product(p, sums):
        result = acc[p] + jnp.dot(ghost[...], ghost_weights[p], preferred_element_type=F32)
        for at in range(2):
            s = 2 * p + at
            mine = result[:, at * count : (at + 1) * count]
            cols_ref[pl.ds(s, modes, stride=snaps), :] = mine
            norm = jnp.sqrt(jnp.sum(mine * mine, axis=0, keepdims=True))
            norm = jnp.sum(norm, axis=1, keepdims=True)
            line = jnp.concatenate([jnp.sum(mine, axis=1, keepdims=True), norm], axis=0)
            sums = jnp.where(lane == s, line, sums)
        return sums

    pairs = snaps // 2
    if pairs <= 4:
        for p in range(pairs):
            own_product(p)
    else:
        lax.fori_loop(0, pairs, lambda p, c: (own_product(p), c)[1], 0)

    ghost_copy.wait_recv()
    for k in range(3):
        if split:
            ghost[:half, k * ghosts : (k + 1) * ghosts] = ghost_in[k, :, :ghosts]
            ghost[half:, k * ghosts : (k + 1) * ghosts] = ghost_in[k, : modes - half, ghosts:]
        else:
            ghost[:, k * ghosts : (k + 1) * ghosts] = ghost_in[k, :modes]
    sums = jnp.zeros((modes + 1, 128), F32)
    if pairs <= 4:
        for p in range(pairs):
            sums = whole_product(p, sums)
    else:
        sums = lax.fori_loop(0, pairs, whole_product, sums)

    wide = part_p.shape[2]
    part[: modes + 1] = sums
    flat = jnp.concatenate(
        [jnp.transpose(part[t * 128 : (t + 1) * 128])[:snaps] for t in range(wide // 128)], axis=1
    )
    waits = sends + [ghost_copy]

    def reduced(value, ref, me, size, device_of, send, recv):
        ref[me] = value
        arriving = []
        for j, (to, source) in enumerate(peers(me, size)):
            out = remote(ref.at[me], ref.at[me], send.at[j], recv.at[me], device_of(to))
            out.start()
            waits.append(out)
            arriving.append(remote(
                ref.at[source], ref.at[source], send.at[j], recv.at[source], device_of(to)
            ))
        for copy in arriving:
            copy.wait_recv()
        total = ref[0]
        for j in range(1, size):
            total = total + ref[j]
        return total

    flat = reduced(flat, part_p, me_p, params, lambda p: (me_e, p), send_p, recv_p)
    flat = reduced(flat, part_i, me_i, inner, inner_id, send_i, recv_i)
    flat = reduced(flat, part_o, me_o, outer, outer_id, send_o, recv_o)
    flat_ref[...] = flat
    for copy in waits:
        copy.wait_send()


def finish_kernel(elem_total, cols_ref, flat_ref, training_hbm, target_hbm, training, target, sem):
    snaps, modes = target.shape
    row_scale = flat_ref[:, modes : modes + 1] / elem_total
    target[...] = flat_ref[:, :modes] / (row_scale * math.sqrt(elem_total))
    copies = [pltpu.make_async_copy(target, target_hbm, sem.at[0])]
    copies[0].start()
    inverse = jnp.broadcast_to(1.0 / row_scale, (snaps, training.shape[2]))
    chunks = sem.shape[0] - 1
    size = modes // chunks
    for c in range(chunks):
        piece = cols_ref[c * size * snaps : (c + 1) * size * snaps]
        piece = piece.reshape(size, snaps, training.shape[2]) * inverse[None]
        training[c * size : (c + 1) * size] = piece.astype(BF16)
        rows = pl.ds(c * size, size)
        copies.append(pltpu.make_async_copy(training.at[rows], training_hbm.at[rows], sem.at[c + 1]))
        copies[-1].start()
    for copy in copies:
        copy.wait()


def local(elems, params, coords, basis_rows, connectivity, modulus, stiffness):
    own_snaps, modes = coords.shape
    nodes = basis_rows.shape[2]
    count = connectivity.shape[0]
    snaps = own_snaps * params
    ghosts = nodes // 4
    inner = 4 if elems % 4 == 0 else elems
    outer = elems // inner
    half, across = (modes, ghosts) if ghosts % 128 == 0 else (round_up(-(-modes // 2), 32), 2 * ghosts)
    tiles = nodes // 128 + -(-ghosts // 128)
    wide = round_up(modes + 1, 128)
    dma = pltpu.SemaphoreType.DMA
    vmem = pl.BlockSpec(memory_space=pltpu.VMEM)
    hbm = pl.BlockSpec(memory_space=pltpu.HBM)
    cols, flat = pl.pallas_call(
        functools.partial(kernel, elems, params, inner),
        out_shape=(
            jax.ShapeDtypeStruct((modes * snaps, count), F32),
            jax.ShapeDtypeStruct((snaps, wide), F32),
        ),
        in_specs=[hbm] * 5,
        out_specs=(vmem, vmem),
        scratch_shapes=[
            pltpu.VMEM((own_snaps, modes), BF16),
            pltpu.VMEM((modes, 3 * nodes), BF16),
            pltpu.VMEM((8, count), jnp.int32),
            pltpu.VMEM((1, count), F32),
            pltpu.VMEM(stiffness.shape, F32),
            pltpu.VMEM((3, round_up(half, 16), across), BF16),
            pltpu.VMEM((3, round_up(half, 16), across), BF16),
            pltpu.VMEM((modes, 3 * ghosts), BF16),
            pltpu.VMEM((params, tiles, 3, own_snaps, 128), F32),
            pltpu.VMEM((nodes + ghosts, count), BF16),
            pltpu.VMEM((3 * nodes, 2 * count), BF16),
            pltpu.VMEM((snaps // 2, 3 * ghosts, 2 * count), BF16),
            pltpu.VMEM((snaps // 2, modes, 2 * count), F32),
            pltpu.VMEM((wide, 128), F32),
            pltpu.VMEM((params, snaps, wide), F32),
            pltpu.VMEM((inner, snaps, wide), F32),
            pltpu.VMEM((outer, snaps, wide), F32),
            dma((7,)), dma, dma,
            dma((params,)), dma((params,)),
            dma((params,)), dma((params,)),
            dma((params,)), dma((params,)),
            dma((inner,)), dma((inner,)),
            dma((outer,)), dma((outer,)),
        ],
        compiler_params=pltpu.CompilerParams(
            collective_id=0, has_side_effects=True, vmem_limit_bytes=44 * 1024 * 1024
        ),
    )(coords, basis_rows, connectivity.T, modulus.reshape(1, count), stiffness)
    chunks = next(c for c in (4, 3, 2, 1) if modes % c == 0)
    training, target = pl.pallas_call(
        functools.partial(finish_kernel, count * elems * params),
        out_shape=(
            jax.ShapeDtypeStruct((modes, snaps, count), BF16),
            jax.ShapeDtypeStruct((snaps, modes), F32),
        ),
        in_specs=[vmem, vmem],
        out_specs=(hbm, hbm),
        scratch_shapes=[
            pltpu.VMEM((modes, snaps, count), BF16),
            pltpu.VMEM((snaps, modes), F32),
            dma((chunks + 1,)),
        ],
        compiler_params=pltpu.CompilerParams(vmem_limit_bytes=20 * 1024 * 1024),
    )(cols, flat)
    return (jnp.transpose(training, (1, 0, 2)), target)


def solution(mesh):
    in_specs = (
        P("param", None),
        P(None, None, "elem"),
        P(("elem", "param"), None),
        P(("elem", "param")),
        P(),
    )
    out_specs = (P(None, None, ("elem", "param")), P())
    run = functools.partial(local, mesh.shape["elem"], mesh.shape["param"])
    return jax.shard_map(run, mesh=mesh, in_specs=in_specs, out_specs=out_specs, check_vma=False)
```

time: 29.7 us -> 27.7 us (0.933)
  local copies, waits for them, and re-layouts: 5.55 us -> 3.75 us
    unnamed x11 -> x10, local copies, waits for them, and re-layouts: 5.43 us -> 3.75 us
    pallas_call x1, Pallas kernels: 23.1 us -> 22 us  [local(): pl.pallas_call(functools.partial(kernel, elems, params, inner), out_shape...]
    pallas_call x0 -> x1, Pallas kernels: none -> 0.96 us  [local(): pl.pallas_call(functools.partial(finish_kernel, count * elems * params),...]
where the time goes in v2:
time: 27.7 us; the launch traced here: 27.4 us
  Pallas kernels  23 us (83%)
  local copies, waits for them, and re-layouts  3.75 us (14%)
  between operations  0.65 us (2%)
    pallas_call x1, Pallas kernels, local(): pl.pallas_call(functools.partial(kernel, elems, params, inner), out_shape...  22 us
    unnamed x10, local copies, waits for them, and re-layouts  3.75 us
    pallas_call x1, Pallas kernels, local(): pl.pallas_call(functools.partial(finish_kernel, count * elems * params),...  0.96 us

profile of v2, /device:TPU:0, one launch (start us, length us, event | category | flops | bytes accessed | tf_op | source)
XLA Modules:
  0.0 27.4 jit_solution(15193732935999632392)
XLA Ops:
  0.6 0.0 copy-start
  0.6 1.0 %copy-done = bf16[3,300,256]{2,1,0:T(8,128)(2,1)S(1)} copy-done((bf16[3,300,256]{2,1,0:T(8,128)(2,1)S(1)}, bf16[3,300,256]{2,1,0:T(8,128)(2,1)}, u32[]{:S(2)}) %copy-start) | copy-done | bytes 460824
  1.7 0.0 copy-start.1
  1.7 0.7 %copy-done.1 = f32[24,24]{1,0:T(8,128)S(1)} copy-done((f32[24,24]{1,0:T(8,128)S(1)}, f32[24,24]{1,0:T(8,128)}, u32[]{:S(2)}) %copy-start.1) | copy-done | bytes 2328
  2.4 0.0 copy-start.2
  2.4 0.7 %copy-done.2 = s32[128,8]{0,1:T(8,128)S(1)} copy-done((s32[128,8]{0,1:T(8,128)S(1)}, s32[128,8]{0,1:T(8,128)}, u32[]{:S(2)}) %copy-start.2) | copy-done | bytes 4120
  3.0 0.0 copy-start.3
  3.1 0.7 %copy-done.3 = bf16[4,300]{1,0:T(4,128)(2,1)S(1)} copy-done((bf16[4,300]{1,0:T(4,128)(2,1)S(1)}, bf16[4,300]{1,0:T(4,128)(2,1)}, u32[]{:S(2)}) %copy-start.3) | copy-done | bytes 2424
  3.7 0.0 copy-start.4
  3.7 0.7 %copy-done.4 = f32[128]{0:T(128)S(1)} copy-done((f32[128]{0:T(128)S(1)}, f32[128]{0:T(128)}, u32[]{:S(2)}) %copy-start.4) | copy-done | bytes 536
  4.4 22.0 %shard_map.68 = (f32[2400,128]{1,0:T(8,128)S(1)}, f32[8,384]{1,0:T(8,128)S(1)}) custom-call(bf16[4,300]{1,0:T(4,128)(2,1)S(1)} %copy-done.3, bf16[3,300,256]{2,1,0:T(8,128)(2,1)S(1)} %copy-done, s32[8,128]{1,0:T(8,128)S(1)} %bitcast.3, f32[1,128]{1,0:T(1,128)S(1)} %bitcast.4, f32[24,24]{1,0:T(8,128)S(1)} %copy-done.1), custom_call_target="tpu_custom_call" | custom-call | tf_op jit(solution)/shard_map/pallas_call | solution.py:272
  26.4 1.0 %shard_map.69 = (bf16[300,8,128]{2,1,0:T(8,128)(2,1)}, f32[8,300]{1,0:T(8,128)}) custom-call(f32[2400,128]{1,0:T(8,128)S(1)} %get-tuple-element.6.cols_ref, f32[8,384]{1,0:T(8,128)S(1)} %get-tuple-element.7.flat_ref), custom_call_target="tpu_custom_call" | custom-call | tf_op jit(solution)/shard_map/pallas_call | solution.py:310
Async XLA Ops:
  0.6 1.0 %copy-start = (bf16[3,300,256]{2,1,0:T(8,128)(2,1)S(1)}, bf16[3,300,256]{2,1,0:T(8,128)(2,1)}, u32[]{:S(2)}) copy-start(bf16[3,300,256]{2,1,0:T(8,128)(2,1)} %basis_hbm.1) | copy-start | bytes 1382404
  1.7 0.7 %copy-start.1 = (f32[24,24]{1,0:T(8,128)S(1)}, f32[24,24]{1,0:T(8,128)}, u32[]{:S(2)}) copy-start(f32[24,24]{1,0:T(8,128)} %stiff_hbm.1) | copy-start | bytes 6916
  2.4 0.7 %copy-start.2 = (s32[128,8]{0,1:T(8,128)S(1)}, s32[128,8]{0,1:T(8,128)}, u32[]{:S(2)}) copy-start(s32[128,8]{0,1:T(8,128)} %param.7) | copy-start | bytes 12292
  3.0 0.7 %copy-start.3 = (bf16[4,300]{1,0:T(4,128)(2,1)S(1)}, bf16[4,300]{1,0:T(4,128)(2,1)}, u32[]{:S(2)}) copy-start(bf16[4,300]{1,0:T(4,128)(2,1)} %coords_hbm.1) | copy-start | bytes 7204
  3.7 0.7 %copy-start.4 = (f32[128]{0:T(128)S(1)}, f32[128]{0:T(128)}, u32[]{:S(2)}) copy-start(f32[128]{0:T(128)} %param.8) | copy-start | bytes 1540

commit v3 on v2

--- a/solution.py
+++ b/solution.py
@@ -19,19 +19,19 @@
 
 def kernel(
     elems, params, inner,
-    coords_hbm, basis_hbm, conn_hbm, mod_hbm, stiff_hbm,
+    own_snaps, modes, dofs,
+    small_ref, basis_hbm,
     cols_ref, flat_ref,
-    coords_ref, basis_ref, conn_ref, mod_ref, stiff_ref,
+    basis_ref,
     packed, ghost_in, ghost, disp, mask, weights, ghost_weights, acc, part, part_p, part_i, part_o,
     load, send_g, recv_g, send_d, recv_d, send_n, recv_n, send_p, recv_p, send_i, recv_i, send_o, recv_o,
 ):
     outer = elems // inner
-    own_snaps, modes = coords_ref.shape
     snaps = own_snaps * params
     nodes = basis_hbm.shape[2]
     ghosts = nodes // 4
     total_nodes = nodes + ghosts
-    count = conn_ref.shape[1]
+    count = cols_ref.shape[1]
     me_e, me_p = lax.axis_index("elem"), lax.axis_index("param")
     me_i, me_o = me_e % inner, me_e // inner
     before, after = (me_e + elems - 1) % elems, (me_e + 1) % elems
@@ -53,10 +53,12 @@
     for device in near:
         pl.semaphore_signal(barrier, inc=1, device_id=device, device_id_type=MESH)
 
-    loads = [(coords_hbm, coords_ref)]
-    loads += [(basis_hbm.at[k], basis_ref.at[:, pl.ds(k * nodes, nodes)]) for k in range(3)]
-    loads += [(conn_hbm, conn_ref), (mod_hbm, mod_ref), (stiff_hbm, stiff_ref)]
-    loads = [pltpu.make_async_copy(src, dst, load.at[i]) for i, (src, dst) in enumerate(loads)]
+    loads = [
+        pltpu.make_async_copy(
+            basis_hbm.at[k], basis_ref.at[:, pl.ds(k * nodes, nodes)], load.at[k]
+        )
+        for k in range(3)
+    ]
     for copy in loads:
         copy.start()
 
@@ -70,11 +72,12 @@
     ghost_tiles = disp.shape[1] - own_tiles
     half = packed.shape[1]
     split = half < modes
-    loads[0].wait()
+    conn_at, mod_at, coords_at = dofs, dofs + 8, dofs + 16
+    coords = small_ref[coords_at : coords_at + own_snaps, :modes].astype(BF16)
     for k in range(3):
-        loads[1 + k].wait()
+        loads[k].wait()
         moved = jnp.dot(
-            coords_ref[...], basis_ref[:, k * nodes : (k + 1) * nodes], preferred_element_type=F32
+            coords, basis_ref[:, k * nodes : (k + 1) * nodes], preferred_element_type=F32
         )
         moved = moved.astype(BF16).astype(F32)
         for t in range(own_tiles):
@@ -114,9 +117,7 @@
     for copy in sends + [ghost_copy]:
         copy.start()
 
-    for copy in loads[4:]:
-        copy.wait()
-    corners = conn_ref[...]
+    corners = small_ref[conn_at : conn_at + 8, :count].astype(jnp.int32)
     base = jnp.min(corners, axis=0, keepdims=True)
     residue = corners % 8
     lane_at = corners % 128
@@ -124,12 +125,12 @@
     node = lax.broadcasted_iota(jnp.int32, (total_nodes, count), 0)
     inside = (node >= base) & (node < base + 8)
     mask[...] = jnp.where(inside, 1.0, 0.0).astype(BF16)
-    stiff = stiff_ref[...]
+    stiff = small_ref[:dofs, :dofs]
     high = stiff.astype(BF16)
     rest = stiff - high.astype(F32)
     mid = rest.astype(BF16)
     low = (rest - mid.astype(F32)).astype(BF16)
-    modulus = mod_ref[...]
+    modulus = small_ref[mod_at : mod_at + 1, :count]
     modulus2 = jnp.concatenate([modulus, modulus], axis=1)
     part[...] = jnp.zeros_like(part)
     lane = lax.broadcasted_iota(jnp.int32, (1, 128), 1)
@@ -269,20 +270,32 @@
     dma = pltpu.SemaphoreType.DMA
     vmem = pl.BlockSpec(memory_space=pltpu.VMEM)
     hbm = pl.BlockSpec(memory_space=pltpu.HBM)
+    dofs = stiffness.shape[0]
+    tall = round_up(own_snaps, 8)
+    pieces = [
+        (stiffness, 0),
+        (connectivity.T, dofs),
+        (modulus[None], dofs + 8),
+        (coords, dofs + 16),
+    ]
+    height, across_small = dofs + 16 + tall, round_up(max(modes, count), 128)
+    small = None
+    for piece, at in pieces:
+        placed = lax.pad(
+            piece, jnp.zeros((), piece.dtype),
+            ((at, height - at - piece.shape[0], 0), (0, across_small - piece.shape[1], 0)),
+        ).astype(F32)
+        small = placed if small is None else small + placed
     cols, flat = pl.pallas_call(
-        functools.partial(kernel, elems, params, inner),
+        functools.partial(kernel, elems, params, inner, own_snaps, modes, dofs),
         out_shape=(
             jax.ShapeDtypeStruct((modes * snaps, count), F32),
             jax.ShapeDtypeStruct((snaps, wide), F32),
         ),
-        in_specs=[hbm] * 5,
+        in_specs=[vmem, hbm],
         out_specs=(vmem, vmem),
         scratch_shapes=[
-            pltpu.VMEM((own_snaps, modes), BF16),
             pltpu.VMEM((modes, 3 * nodes), BF16),
-            pltpu.VMEM((8, count), jnp.int32),
-            pltpu.VMEM((1, count), F32),
-            pltpu.VMEM(stiffness.shape, F32),
             pltpu.VMEM((3, round_up(half, 16), across), BF16),
             pltpu.VMEM((3, round_up(half, 16), across), BF16),
             pltpu.VMEM((modes, 3 * ghosts), BF16),
@@ -295,7 +308,7 @@
             pltpu.VMEM((params, snaps, wide), F32),
             pltpu.VMEM((inner, snaps, wide), F32),
             pltpu.VMEM((outer, snaps, wide), F32),
-            dma((7,)), dma, dma,
+            dma((3,)), dma, dma,
             dma((params,)), dma((params,)),
             dma((params,)), dma((params,)),
             dma((params,)), dma((params,)),
@@ -305,7 +318,7 @@
         compiler_params=pltpu.CompilerParams(
             collective_id=0, has_side_effects=True, vmem_limit_bytes=44 * 1024 * 1024
         ),
-    )(coords, basis_rows, connectivity.T, modulus.reshape(1, count), stiffness)
+    )(small, basis_rows)
     chunks = next(c for c in (4, 3, 2, 1) if modes % c == 0)
     training, target = pl.pallas_call(
         functools.partial(finish_kernel, count * elems * params),

time: 27.7 us -> 25.6 us (0.924)
  local copies, waits for them, and re-layouts: 3.75 us -> 1.02 us
  other arithmetic: 0 us -> 0.75 us
    unnamed x10 -> x2, local copies, waits for them, and re-layouts: 3.75 us -> 1.02 us
    add x0 -> x1, other arithmetic: none -> 0.75 us  [local(): small = placed if small is None else small + placed]
where the time goes in v3:
time: 25.6 us; the launch traced here: 25.4 us
  Pallas kernels  22.9 us (89%)
  local copies, waits for them, and re-layouts  1.02 us (4%)
  other arithmetic  0.75 us (3%)
  between operations  0.65 us (3%)
    pallas_call x1, Pallas kernels, local(): pl.pallas_call(functools.partial(kernel, elems, params, inner, own_snaps,...  22 us
    unnamed x2, local copies, waits for them, and re-layouts  1.02 us
    pallas_call x1, Pallas kernels, local(): pl.pallas_call(functools.partial(finish_kernel, count * elems * params),...  0.96 us
    add x1, other arithmetic, local(): small = placed if small is None else small + placed  0.75 us

profile of v3, /device:TPU:0, one launch (start us, length us, event | category | flops | bytes accessed | tf_op | source)
XLA Modules:
  0.0 25.4 jit_solution(11822997968967597844)
XLA Ops:
  0.6 0.7 %convert_add_fusion.small_ref = f32[48,384]{1,0:T(8,128)S(1)} fusion(f32[1,128]{1,0:T(1,128)} %bitcast.4, s32[8,128]{1,0:T(8,128)} %bitcast.3, f32[24,24]{1,0:T(8,128)} %param.9, bf16[4,300]{1,0:T(4,128)(2,1)} %param.5), kind=kLoop, calls=%fused_computation | loop fusion | flops 92160 | bytes 83040 | tf_op jit(solution)/shard_map/add | solution.py:288
  1.4 0.0 copy-start
  1.4 1.0 %copy-done = bf16[3,300,256]{2,1,0:T(8,128)(2,1)S(1)} copy-done((bf16[3,300,256]{2,1,0:T(8,128)(2,1)S(1)}, bf16[3,300,256]{2,1,0:T(8,128)(2,1)}, u32[]{:S(2)}) %copy-start) | copy-done | bytes 460824
  2.4 22.0 %shard_map.68 = (f32[2400,128]{1,0:T(8,128)S(1)}, f32[8,384]{1,0:T(8,128)S(1)}) custom-call(f32[48,384]{1,0:T(8,128)S(1)} %convert_add_fusion.small_ref, bf16[3,300,256]{2,1,0:T(8,128)(2,1)S(1)} %copy-done), custom_call_target="tpu_custom_call" | custom-call | tf_op jit(solution)/shard_map/pallas_call | solution.py:289
  24.4 1.0 %shard_map.69 = (bf16[300,8,128]{2,1,0:T(8,128)(2,1)}, f32[8,300]{1,0:T(8,128)}) custom-call(f32[2400,128]{1,0:T(8,128)S(1)} %get-tuple-element.6.cols_ref, f32[8,384]{1,0:T(8,128)S(1)} %get-tuple-element.7.flat_ref), custom_call_target="tpu_custom_call" | custom-call | tf_op jit(solution)/shard_map/pallas_call | solution.py:323
Async XLA Ops:
  1.4 1.0 %copy-start = (bf16[3,300,256]{2,1,0:T(8,128)(2,1)S(1)}, bf16[3,300,256]{2,1,0:T(8,128)(2,1)}, u32[]{:S(2)}) copy-start(bf16[3,300,256]{2,1,0:T(8,128)(2,1)} %basis_hbm.1) | copy-start | bytes 1382404
